TPU v7x, 32 devices: a whole 2x2x4 slice. The times are simulated.
32 devices in a mesh: rows: 8 (over z, x), feat: 4 (over y, core).
Axes of the slice: x: 2, y: 2, z: 4, core: 2. Of those that a mesh axis runs over, the one named last changes fastest.
Arguments:
- tile_values: bfloat16 [2048, 256, 128], P('rows', 'feat'), may hold values from -6 to 6
- tile_blocks: int32 [2048, 256], P('rows', 'feat'), may hold values from 0 to 2047
- tile_counts: int32 [2048, 4], P('rows', 'feat'), may hold values from 1 to 64, as said below
- labels: int32 [2048], P('rows'), may hold values 0 or 1
- owner_rank: int32 [2048], P('rows'), may hold values from 0 to 7, as said below
- weights: float32 [8192, 128], P(('feat', 'rows')), may hold values from -0.09375 to 0.09375
Outputs:
- owned_margins: float32 [2048], P('rows')
- gradient: float32 [8192, 128], P(('feat', 'rows'))
- loss: float32 [], replicated
Inputs may be any that keep to these rules, and one draw needn't show every extreme that they name: `owner_rank`: within each aligned block of 256 examples, every owner is named by exactly 32 examples. `tile_counts`: in every aligned block of 256 examples, each shard's column holds at least one example with exactly 64 used slots.
All inputs are finite; a program needn't handle non-finite values. No bound on the sum of `labels` on one device may be relied on, other than what follows from the above.
Results may differ from a plain program's by a relative error of at most 0.003.
Values may be sent and summed in bfloat16 or wider, within the bound.
A program may use at most 64 MiB of HBM per device.

v0:
```python
import math

import jax
import jax.numpy as jnp
from jax import lax
from jax.sharding import PartitionSpec as P


def on_device(tile_values, tile_blocks, tile_counts, labels, owner_rank, weights):
    examples = tile_values.shape[0]
    slot_count = tile_values.shape[1]
    tile_width = tile_values.shape[2]
    peer_count = lax.axis_size("rows")
    per_owner = examples // peer_count
    w_half = weights.astype(jnp.bfloat16)
    weight_table = lax.all_gather(w_half, "rows", axis=0, tiled=True)
    owner_hits = (owner_rank[:, None] == jnp.arange(peer_count, dtype=jnp.int32)[None, :]).astype(
        jnp.int32
    )
    earlier = jnp.cumsum(owner_hits, axis=0) - owner_hits
    local_rank = jnp.sum(earlier * owner_hits, axis=1)
    position = owner_rank * per_owner + local_rank
    send_order = (
        jnp.zeros((examples,), jnp.int32).at[position].set(jnp.arange(examples, dtype=jnp.int32))
    )
    counts_here = tile_counts[:, 0]
    live_slot = jnp.arange(slot_count, dtype=jnp.int32)[None, :] < counts_here[:, None]
    picked = weight_table[tile_blocks]
    products = jnp.sum(tile_values.astype(jnp.float32) * picked.astype(jnp.float32), axis=2)
    partial_value = jnp.sum(jnp.where(live_slot, products, jnp.float32(0.0)), axis=1)
    margin = lax.psum(partial_value, "feat")
    label_float = labels.astype(jnp.float32)
    residual = jax.nn.sigmoid(margin) - label_float
    loss_terms = jnp.sum(jax.nn.softplus(margin) - label_float * margin)
    loss = lax.psum(loss_terms, "rows") / (examples * peer_count)
    resid_half = residual.astype(jnp.bfloat16)
    coefficient = jnp.where(live_slot, resid_half[:, None], jnp.zeros((), jnp.bfloat16))
    total_tiles = examples * slot_count
    block_rows = math.gcd(total_tiles, 1024)
    turn_count = total_tiles // block_rows
    flat_values = tile_values.reshape(turn_count, block_rows, tile_width)
    flat_blocks = tile_blocks.reshape(turn_count, block_rows)
    flat_coefficient = coefficient.reshape(turn_count, block_rows)
    row_count = weights.shape[0] * lax.axis_size("rows")
    candidates = jnp.arange(row_count, dtype=jnp.int32)

    def add_block(running, pieces):
        block_values, block_ids, block_coefficient = pieces
        matches = block_ids[:, None] == candidates[None, :]
        spread = jnp.where(matches, block_coefficient[:, None], jnp.zeros((), jnp.bfloat16))
        update = lax.dot_general(
            spread, block_values, (((0,), (0,)), ((), ())), preferred_element_type=jnp.float32
        )
        return (running + update, None)

    start_sum = jnp.zeros((row_count, tile_width), jnp.float32)
    summed, unused = lax.scan(add_block, start_sum, (flat_values, flat_blocks, flat_coefficient))
    gradient = lax.psum_scatter(summed, "rows", scatter_dimension=0, tiled=True)
    ordered = margin[send_order].reshape(peer_count, per_owner)
    owned_margins = lax.all_to_all(
        ordered, "rows", split_axis=0, concat_axis=0, tiled=True
    ).reshape(examples)
    return (owned_margins, gradient, loss)


def solution(mesh):
    in_specs = (
        P("rows", "feat", None),
        P("rows", "feat"),
        P("rows", "feat"),
        P("rows"),
        P("rows"),
        P(("feat", "rows"), None),
    )
    out_specs = (P("rows"), P(("feat", "rows"), None), P())
    return jax.shard_map(
        on_device, mesh=mesh, in_specs=in_specs, out_specs=out_specs, check_vma=False
    )
```

profile of v0, /device:TPU:0, one launch (start us, length us, event | category | flops | bytes accessed | tf_op | source)
XLA Modules:
  0.0 238.3 jit_solution(4810306240248693229)
XLA Ops:
  9.9 33.0 %all_gather.3 = bf16[2048,128]{1,0:T(8,128)(2,1)S(1)} all-gather(bf16[256,128]{1,0:T(8,128)(2,1)S(1)} %convert_element_type.23), channel_id=1, replica_groups=mesh['rows'=8,'feat'=4] {'rows'}, dimensions={0}, use_global_device_ids=true | all-gather | bytes 589824 | tf_op jit(solution)/shard_map/all_gather | solution.py:16
  43.2 57.4 %gather_fusion = bf16[16384,128]{1,0:T(8,128)(2,1)} fusion(bf16[2048,128]{1,0:T(8,128)(2,1)S(1)} %all_gather.3, s32[16384]{0:T(1024)S(1)} %broadcast_clamp_fusion), kind=kCustom, calls=%fused_computation | custom fusion | bytes 8454144 | tf_op jit(solution)/shard_map/gather | solution.py:28
  100.6 5.7 %fusion.15 = f32[256,64]{1,0:T(8,128)S(1)} fusion(bf16[256,64,128]{2,1,0:T(8,128)(2,1)} %bitcast.22, bf16[256,64,128]{2,1,0:T(8,128)(2,1)} %param.8), kind=kLoop, calls=%fused_computation.18 | loop fusion | flops 8372224 | bytes 8454144 | tf_op jit(solution)/shard_map/reduce_sum | solution.py:29
  106.5 5.7 %psum.14 = f32[256]{0:T(256)S(1)} all-reduce(f32[256]{0:T(256)S(1)} %select_reduce_fusion), channel_id=1, replica_groups=mesh['rows'=8,'feat'=4] {'feat'}, use_global_device_ids=true, to_apply=%region_2.3 | all-reduce | flops 256 | bytes 2048 | tf_op jit(solution)/shard_map/psum | solution.py:31
  114.8 48.5 %while.11 = (s32[]{:T(128)}, f32[2048,128]{1,0:T(8,128)S(1)}, s32[16,1024]{1,0:T(8,128)S(1)}, bf16[16,1024]{1,0:T(8,128)(2,1)S(1)}, bf16[16,1024,128]{2,1,0:T(8,128)(2,1)}, /*index=5*/s32[]{:T(128)}, s32[]{:T(128)}) while((s32[]{:T(128)}, f32[2048,128]{1,0:T(8,128)S(1)}, s32[16,1024]{1,0:T(8,128)S(1)}, ...), condition=%wide.region_8.9_spmd.clone, body=%wide.region_7.8_spmd.clone.sunk | while | flops 541589504 | bytes 2377835 | solution.py:57
  114.8 3.0 %fusion.29 = f32[2048,128]{1,0:T(8,128)S(1)} fusion(s32[1024]{0:T(1024)S(1)} %bitcast.24, bf16[1024]{0:T(1024)(128)(2,1)S(1)} %dynamic-slice_reduce_fusion.2, f32[2048,128]{1,0:T(8,128)S(1)} %get-tuple-element.107, pred[]{:T(512)S(6)} %compare.3, bf16[16,1024,128]{2,1,0:T(8,128)(2,1)} %get-tuple-element.117, s32[]{:T(128)S(6)} %copy.20), kind=kOutput, calls=%fused_computation.8.clone.1 | convolution fusion | flops 541589504 | bytes 2365445 | tf_op jit(solution)/shard_map/while/body/eval_jaxpr/dot_general | solution.py:51
  117.9 3.0 %fusion.29 = f32[2048,128]{1,0:T(8,128)S(1)} fusion(s32[1024]{0:T(1024)S(1)} %bitcast.24, bf16[1024]{0:T(1024)(128)(2,1)S(1)} %dynamic-slice_reduce_fusion.2, f32[2048,128]{1,0:T(8,128)S(1)} %get-tuple-element.107, pred[]{:T(512)S(6)} %compare.3, bf16[16,1024,128]{2,1,0:T(8,128)(2,1)} %get-tuple-element.117, s32[]{:T(128)S(6)} %copy.20), kind=kOutput, calls=%fused_computation.8.clone.1 | convolution fusion | flops 541589504 | bytes 2365445 | tf_op jit(solution)/shard_map/while/body/eval_jaxpr/dot_general | solution.py:51
  120.9 3.0 %fusion.29 = f32[2048,128]{1,0:T(8,128)S(1)} fusion(s32[1024]{0:T(1024)S(1)} %bitcast.24, bf16[1024]{0:T(1024)(128)(2,1)S(1)} %dynamic-slice_reduce_fusion.2, f32[2048,128]{1,0:T(8,128)S(1)} %get-tuple-element.107, pred[]{:T(512)S(6)} %compare.3, bf16[16,1024,128]{2,1,0:T(8,128)(2,1)} %get-tuple-element.117, s32[]{:T(128)S(6)} %copy.20), kind=kOutput, calls=%fused_computation.8.clone.1 | convolution fusion | flops 541589504 | bytes 2365445 | tf_op jit(solution)/shard_map/while/body/eval_jaxpr/dot_general | solution.py:51
  123.9 3.0 %fusion.29 = f32[2048,128]{1,0:T(8,128)S(1)} fusion(s32[1024]{0:T(1024)S(1)} %bitcast.24, bf16[1024]{0:T(1024)(128)(2,1)S(1)} %dynamic-slice_reduce_fusion.2, f32[2048,128]{1,0:T(8,128)S(1)} %get-tuple-element.107, pred[]{:T(512)S(6)} %compare.3, bf16[16,1024,128]{2,1,0:T(8,128)(2,1)} %get-tuple-element.117, s32[]{:T(128)S(6)} %copy.20), kind=kOutput, calls=%fused_computation.8.clone.1 | convolution fusion | flops 541589504 | bytes 2365445 | tf_op jit(solution)/shard_map/while/body/eval_jaxpr/dot_general | solution.py:51
  127.0 3.0 %fusion.29 = f32[2048,128]{1,0:T(8,128)S(1)} fusion(s32[1024]{0:T(1024)S(1)} %bitcast.24, bf16[1024]{0:T(1024)(128)(2,1)S(1)} %dynamic-slice_reduce_fusion.2, f32[2048,128]{1,0:T(8,128)S(1)} %get-tuple-element.107, pred[]{:T(512)S(6)} %compare.3, bf16[16,1024,128]{2,1,0:T(8,128)(2,1)} %get-tuple-element.117, s32[]{:T(128)S(6)} %copy.20), kind=kOutput, calls=%fused_computation.8.clone.1 | convolution fusion | flops 541589504 | bytes 2365445 | tf_op jit(solution)/shard_map/while/body/eval_jaxpr/dot_general | solution.py:51
  130.0 3.0 %fusion.29 = f32[2048,128]{1,0:T(8,128)S(1)} fusion(s32[1024]{0:T(1024)S(1)} %bitcast.24, bf16[1024]{0:T(1024)(128)(2,1)S(1)} %dynamic-slice_reduce_fusion.2, f32[2048,128]{1,0:T(8,128)S(1)} %get-tuple-element.107, pred[]{:T(512)S(6)} %compare.3, bf16[16,1024,128]{2,1,0:T(8,128)(2,1)} %get-tuple-element.117, s32[]{:T(128)S(6)} %copy.20), kind=kOutput, calls=%fused_computation.8.clone.1 | convolution fusion | flops 541589504 | bytes 2365445 | tf_op jit(solution)/shard_map/while/body/eval_jaxpr/dot_general | solution.py:51
  133.0 3.0 %fusion.29 = f32[2048,128]{1,0:T(8,128)S(1)} fusion(s32[1024]{0:T(1024)S(1)} %bitcast.24, bf16[1024]{0:T(1024)(128)(2,1)S(1)} %dynamic-slice_reduce_fusion.2, f32[2048,128]{1,0:T(8,128)S(1)} %get-tuple-element.107, pred[]{:T(512)S(6)} %compare.3, bf16[16,1024,128]{2,1,0:T(8,128)(2,1)} %get-tuple-element.117, s32[]{:T(128)S(6)} %copy.20), kind=kOutput, calls=%fused_computation.8.clone.1 | convolution fusion | flops 541589504 | bytes 2365445 | tf_op jit(solution)/shard_map/while/body/eval_jaxpr/dot_general | solution.py:51
  136.1 3.0 %fusion.29 = f32[2048,128]{1,0:T(8,128)S(1)} fusion(s32[1024]{0:T(1024)S(1)} %bitcast.24, bf16[1024]{0:T(1024)(128)(2,1)S(1)} %dynamic-slice_reduce_fusion.2, f32[2048,128]{1,0:T(8,128)S(1)} %get-tuple-element.107, pred[]{:T(512)S(6)} %compare.3, bf16[16,1024,128]{2,1,0:T(8,128)(2,1)} %get-tuple-element.117, s32[]{:T(128)S(6)} %copy.20), kind=kOutput, calls=%fused_computation.8.clone.1 | convolution fusion | flops 541589504 | bytes 2365445 | tf_op jit(solution)/shard_map/while/body/eval_jaxpr/dot_general | solution.py:51
  139.1 3.0 %fusion.29 = f32[2048,128]{1,0:T(8,128)S(1)} fusion(s32[1024]{0:T(1024)S(1)} %bitcast.24, bf16[1024]{0:T(1024)(128)(2,1)S(1)} %dynamic-slice_reduce_fusion.2, f32[2048,128]{1,0:T(8,128)S(1)} %get-tuple-element.107, pred[]{:T(512)S(6)} %compare.3, bf16[16,1024,128]{2,1,0:T(8,128)(2,1)} %get-tuple-element.117, s32[]{:T(128)S(6)} %copy.20), kind=kOutput, calls=%fused_computation.8.clone.1 | convolution fusion | flops 541589504 | bytes 2365445 | tf_op jit(solution)/shard_map/while/body/eval_jaxpr/dot_general | solution.py:51
  142.1 3.0 %fusion.29 = f32[2048,128]{1,0:T(8,128)S(1)} fusion(s32[1024]{0:T(1024)S(1)} %bitcast.24, bf16[1024]{0:T(1024)(128)(2,1)S(1)} %dynamic-slice_reduce_fusion.2, f32[2048,128]{1,0:T(8,128)S(1)} %get-tuple-element.107, pred[]{:T(512)S(6)} %compare.3, bf16[16,1024,128]{2,1,0:T(8,128)(2,1)} %get-tuple-element.117, s32[]{:T(128)S(6)} %copy.20), kind=kOutput, calls=%fused_computation.8.clone.1 | convolution fusion | flops 541589504 | bytes 2365445 | tf_op jit(solution)/shard_map/while/body/eval_jaxpr/dot_general | solution.py:51
  145.2 3.0 %fusion.29 = f32[2048,128]{1,0:T(8,128)S(1)} fusion(s32[1024]{0:T(1024)S(1)} %bitcast.24, bf16[1024]{0:T(1024)(128)(2,1)S(1)} %dynamic-slice_reduce_fusion.2, f32[2048,128]{1,0:T(8,128)S(1)} %get-tuple-element.107, pred[]{:T(512)S(6)} %compare.3, bf16[16,1024,128]{2,1,0:T(8,128)(2,1)} %get-tuple-element.117, s32[]{:T(128)S(6)} %copy.20), kind=kOutput, calls=%fused_computation.8.clone.1 | convolution fusion | flops 541589504 | bytes 2365445 | tf_op jit(solution)/shard_map/while/body/eval_jaxpr/dot_general | solution.py:51
  148.2 3.0 %fusion.29 = f32[2048,128]{1,0:T(8,128)S(1)} fusion(s32[1024]{0:T(1024)S(1)} %bitcast.24, bf16[1024]{0:T(1024)(128)(2,1)S(1)} %dynamic-slice_reduce_fusion.2, f32[2048,128]{1,0:T(8,128)S(1)} %get-tuple-element.107, pred[]{:T(512)S(6)} %compare.3, bf16[16,1024,128]{2,1,0:T(8,128)(2,1)} %get-tuple-element.117, s32[]{:T(128)S(6)} %copy.20), kind=kOutput, calls=%fused_computation.8.clone.1 | convolution fusion | flops 541589504 | bytes 2365445 | tf_op jit(solution)/shard_map/while/body/eval_jaxpr/dot_general | solution.py:51
  151.2 3.0 %fusion.29 = f32[2048,128]{1,0:T(8,128)S(1)} fusion(s32[1024]{0:T(1024)S(1)} %bitcast.24, bf16[1024]{0:T(1024)(128)(2,1)S(1)} %dynamic-slice_reduce_fusion.2, f32[2048,128]{1,0:T(8,128)S(1)} %get-tuple-element.107, pred[]{:T(512)S(6)} %compare.3, bf16[16,1024,128]{2,1,0:T(8,128)(2,1)} %get-tuple-element.117, s32[]{:T(128)S(6)} %copy.20), kind=kOutput, calls=%fused_computation.8.clone.1 | convolution fusion | flops 541589504 | bytes 2365445 | tf_op jit(solution)/shard_map/while/body/eval_jaxpr/dot_general | solution.py:51
  154.3 3.0 %fusion.29 = f32[2048,128]{1,0:T(8,128)S(1)} fusion(s32[1024]{0:T(1024)S(1)} %bitcast.24, bf16[1024]{0:T(1024)(128)(2,1)S(1)} %dynamic-slice_reduce_fusion.2, f32[2048,128]{1,0:T(8,128)S(1)} %get-tuple-element.107, pred[]{:T(512)S(6)} %compare.3, bf16[16,1024,128]{2,1,0:T(8,128)(2,1)} %get-tuple-element.117, s32[]{:T(128)S(6)} %copy.20), kind=kOutput, calls=%fused_computation.8.clone.1 | convolution fusion | flops 541589504 | bytes 2365445 | tf_op jit(solution)/shard_map/while/body/eval_jaxpr/dot_general | solution.py:51
  157.3 3.0 %fusion.29 = f32[2048,128]{1,0:T(8,128)S(1)} fusion(s32[1024]{0:T(1024)S(1)} %bitcast.24, bf16[1024]{0:T(1024)(128)(2,1)S(1)} %dynamic-slice_reduce_fusion.2, f32[2048,128]{1,0:T(8,128)S(1)} %get-tuple-element.107, pred[]{:T(512)S(6)} %compare.3, bf16[16,1024,128]{2,1,0:T(8,128)(2,1)} %get-tuple-element.117, s32[]{:T(128)S(6)} %copy.20), kind=kOutput, calls=%fused_computation.8.clone.1 | convolution fusion | flops 541589504 | bytes 2365445 | tf_op jit(solution)/shard_map/while/body/eval_jaxpr/dot_general | solution.py:51
  160.3 3.0 %fusion.29 = f32[2048,128]{1,0:T(8,128)S(1)} fusion(s32[1024]{0:T(1024)S(1)} %bitcast.24, bf16[1024]{0:T(1024)(128)(2,1)S(1)} %dynamic-slice_reduce_fusion.2, f32[2048,128]{1,0:T(8,128)S(1)} %get-tuple-element.107, pred[]{:T(512)S(6)} %compare.3, bf16[16,1024,128]{2,1,0:T(8,128)(2,1)} %get-tuple-element.117, s32[]{:T(128)S(6)} %copy.20), kind=kOutput, calls=%fused_computation.8.clone.1 | convolution fusion | flops 541589504 | bytes 2365445 | tf_op jit(solution)/shard_map/while/body/eval_jaxpr/dot_general | solution.py:51
  169.3 5.6 %all-to-all-start = ((f32[8,1,32]{2,1,0:T(1,128)}), f32[8,1,32]{2,1,0:T(1,128)S(1)}, u32[]{:S(2)}, u32[]{:S(2)}) async-start(f32[8,1,32]{2,1,0:T(1,128)} %all_to_all.6), calls=%async_computation | async-start | bytes 8192 | tf_op jit(solution)/shard_map/all_to_all | solution.py:60
  175.0 22.5 %psum.15 = f32[]{:T(128)} all-reduce(f32[]{:T(128)} %get-tuple-element.66), channel_id=1, replica_groups=mesh['rows'=8,'feat'=4] {'rows'}, use_global_device_ids=true, to_apply=%region_11.12 | all-reduce | flops 1 | bytes 8 | tf_op jit(solution)/shard_map/psum | solution.py:35
  199.9 30.4 %reduce-scatter.2.cloned.1.call-done = f32[256,128]{1,0:T(8,128)} async-done(((f32[2048,128]{1,0:T(8,128)}), f32[256,128]{1,0:T(8,128)}) %reduce-scatter.2.cloned.1.call-update) | async-done | bytes 131088 | tf_op jit(solution)/shard_map/reduce_scatter | solution.py:58
  (80 shorter events, 14.1 us)
Async XLA Ops:
  7.2 223.2 %reduce-scatter.2.cloned.1.call-start = ((), (), s32[]{:S(2)}) async-start(), calls=%async_computation.2 | async-start | bytes 1179648 | tf_op jit(solution)/shard_map/reduce_scatter | solution.py:58
  100.6 5.7 %copy-start.2 = (s32[256,1]{0,1:T(1,128)S(1)}, s32[256,1]{0,1:T(1,128)}, u32[]{:S(2)}) copy-start(s32[256,1]{0,1:T(1,128)} %param.10) | copy-start | bytes 3076
  100.6 11.7 %copy-start.3 = (s32[256]{0:T(256)S(1)}, s32[256]{0:T(256)}, u32[]{:S(2)}) copy-start(s32[256]{0:T(256)} %param.11) | copy-start | bytes 3076
  114.8 49.5 %copy-start.1 = (s32[256]{0:T(256)S(1)}, s32[256]{0:T(256)}, u32[]{:S(2)}) copy-start(s32[256]{0:T(256)} %param.12) | copy-start | bytes 3076
  163.3 1.0 copy-start
  169.3 28.8 %all-to-all-start = ((f32[8,1,32]{2,1,0:T(1,128)}), f32[8,1,32]{2,1,0:T(1,128)S(1)}, u32[]{:S(2)}, u32[]{:S(2)}) async-start(f32[8,1,32]{2,1,0:T(1,128)} %all_to_all.6), calls=%async_computation | async-start | bytes 8192 | tf_op jit(solution)/shard_map/all_to_all | solution.py:60
Sparse Core Ops, SparseCore 0:
  164.4 65.8 reduce-scatter.1
where the time goes:
time: 239 us; the launch traced here: 238 us
  local copies, waits for them, and re-layouts  66.9 us (28%)
  blocking collectives  61.2 us (26%)
  matrix products  47.2 us (20%)
  waiting for transfers between devices  30.4 us (13%)
  between operations  16 us (7%)
  other arithmetic  10.4 us (4%)
  starting transfers between devices  5.67 us (2%)
    gather x1, local copies, waits for them, and re-layouts, on_device(): picked = weight_table[tile_blocks]  57.4 us
    dot_general x16, matrix products, add_block(): lax.dot_general(spread, block_values, (((0,), (0,)), ((), ())), preferred...  47.2 us
    all_gather x1, blocking collectives, on_device(): weight_table = lax.all_gather(w_half, 'rows', axis=0, tiled=True)  33 us
    reduce_scatter x1, waiting for transfers between devices, on_device(): gradient = lax.psum_scatter(summed, 'rows', scatter_dimension=0, tiled=True)  30.4 us
    psum x1, blocking collectives, on_device(): loss = lax.psum(loss_terms, 'rows') / (examples * peer_count)  22.5 us
    reduce_sum x1, other arithmetic, on_device(): jnp.sum(tile_values.astype(jnp.float32) * picked.astype(jnp.float32), axi...  5.72 us
    psum x1, blocking collectives, on_device(): margin = lax.psum(partial_value, 'feat')  5.66 us
    all_to_all x1, starting transfers between devices, on_device(): lax.all_to_all(ordered, 'rows', split_axis=0, concat_axis=0, tiled=True)  5.63 us
  transfers between devices with their start and end apart: 2, of which 1 were waited for; matrix products, arithmetic and copies ran while one was open for 3% of the time, Pallas kernels for 0%

commit v1 on v0

v1 whole, which is shorter than its diff:
```python
import functools

import jax
import jax.numpy as jnp
from jax import lax
from jax.experimental import pallas as pl
from jax.experimental.pallas import tpu as pltpu
from jax.sharding import PartitionSpec as P

MESH = pl.DeviceIdType.MESH
LANES = 128
GRAIN = 16
GROUP = 16
CHUNK = 256
NT = (((1,), (1,)), ((), ()))
NN = (((1,), (0,)), ((), ()))
VM = pl.BlockSpec(memory_space=pltpu.VMEM)
SM = pl.BlockSpec(memory_space=pltpu.SMEM)


def greet(axis, count):
    me = lax.axis_index(axis)
    barrier = pltpu.get_barrier_semaphore()
    for k in range(1, count):
        peer = lax.rem(me + k, count)
        pl.semaphore_signal(barrier, inc=1, device_id={axis: peer}, device_id_type=MESH)
    pl.semaphore_wait(barrier, count - 1)
    return me


def gather_kernel(n, w_ref, table_ref, half, send, recv):
    rows = w_ref.shape[0]
    half[...] = w_ref[...].astype(jnp.bfloat16)
    me = greet("rows", n)
    here = pl.ds(pl.multiple_of(me * rows, rows), rows)
    copies = []
    for k in range(1, n):
        copy = pltpu.make_async_remote_copy(
            src_ref=half,
            dst_ref=table_ref.at[here],
            send_sem=send.at[k - 1],
            recv_sem=recv.at[k - 1],
            device_id={"rows": lax.rem(me + k, n)},
            device_id_type=MESH,
        )
        copy.start()
        copies.append(copy)
    table_ref[here, :] = w_ref[...].astype(jnp.bfloat16)
    for copy in copies:
        copy.wait()


def lane_group():
    return lax.broadcasted_iota(jnp.int32, (1, LANES), 1) // GRAIN


def group_values(vals_ref, glist, base):
    return jnp.concatenate([vals_ref[glist[base + i]] for i in range(GROUP)], axis=0)


def group_offsets(idt, rlist, base):
    group = lane_group()
    per = LANES // GRAIN
    parts = []
    for h in range(GROUP // per):
        row = idt[pl.ds(rlist[base + h * per], 1), :]
        for i in range(1, per):
            row = jnp.where(group == i, idt[pl.ds(rlist[base + h * per + i], 1), :], row)
        parts.append(row)
    ids = jnp.concatenate(parts, axis=1)
    width = GROUP * GRAIN
    return jnp.broadcast_to(ids, (8, width)) - lax.broadcasted_iota(jnp.int32, (8, width), 0)


def margin_kernel(counts, used_ref, ids_ref, table_ref, vals_ref, glist, rlist, nb, idt, partial_ref, terms):
    ex, slots = ids_ref.shape
    grains = slots // GRAIN
    live = lax.broadcasted_iota(jnp.int32, (ex, slots), 1) < used_ref[...]
    shifted = jnp.where(live, ids_ref[...] + 1, 0)
    if slots < LANES:
        shifted = jnp.concatenate([shifted, jnp.zeros((ex, LANES - slots), jnp.int32)], axis=1)
    lane = lax.broadcasted_iota(jnp.int32, (ex, LANES), 1) // GRAIN
    for q in range(grains):
        piece = jnp.where(lane == q, shifted, 0)
        step = GRAIN
        while step < LANES:
            piece = piece + pltpu.roll(piece, step, 1)
            step *= 2
        idt[q * ex : (q + 1) * ex, :] = piece - 1
    idt[grains * ex :, :] = jnp.full((8, LANES), -1, jnp.int32)

    def fill(e, off):
        for q in range(grains):
            glist[off + q] = e * grains + q
            rlist[off + q] = e + q * ex
        return off + (counts[e] + (GRAIN - 1)) // GRAIN

    total = lax.fori_loop(0, ex, fill, jnp.int32(0), unroll=8)
    for i in range(GROUP):
        glist[total + i] = 0
        rlist[total + i] = grains * ex
    turns = (total + (GROUP - 1)) // GROUP
    nb[0] = turns
    terms[...] = jnp.zeros_like(terms)
    group = lane_group()
    width = GROUP * GRAIN
    per = LANES // GRAIN

    def turn(t, carry):
        base = t * GROUP
        values = group_values(vals_ref, glist, base)
        offset = group_offsets(idt, rlist, base)
        found = jnp.zeros((8, width), jnp.float32)
        for c in range(table_ref.shape[0] // CHUNK):
            scores = lax.dot_general(
                table_ref[c * CHUNK : (c + 1) * CHUNK, :], values, NT, preferred_element_type=jnp.float32
            )
            for i in range(CHUNK // 8):
                found = jnp.where(offset == c * CHUNK + i * 8, scores[i * 8 : i * 8 + 8, :], found)
        term = jnp.sum(found, axis=0, keepdims=True)
        for i in range(GROUP):
            h = i // per
            mine = jnp.where(group == i % per, term[:, h * LANES : (h + 1) * LANES], 0.0)
            terms[pl.ds(rlist[base + i], 1), :] = mine
        return carry

    lax.fori_loop(0, turns, turn, jnp.int32(0))
    spread = terms[0:ex, :]
    for q in range(1, grains):
        spread = spread + terms[q * ex : (q + 1) * ex, :]
    partial_ref[...] = jnp.broadcast_to(jnp.sum(spread.T, axis=0, keepdims=True), partial_ref.shape)


def residual_kernel(n, partial_ref, labels_ref, margin_ref, resid_ref, loss_ref, held, send, recv):
    me = greet("feat", n)
    copies = []
    for k in range(1, n):
        copy = pltpu.make_async_remote_copy(
            src_ref=partial_ref,
            dst_ref=held.at[me],
            send_sem=send.at[k - 1],
            recv_sem=recv.at[k - 1],
            device_id={"feat": lax.rem(me + k, n)},
            device_id_type=MESH,
        )
        copy.start()
        copies.append(copy)
    held[me] = partial_ref[...]
    for copy in copies:
        copy.wait()
    margin = held[0]
    for k in range(1, n):
        margin = margin + held[k]
    label = labels_ref[...].astype(jnp.float32)
    residual = 1.0 / (1.0 + jnp.exp(-margin)) - label
    margin_ref[...] = margin
    resid_ref[...] = residual.astype(jnp.bfloat16).astype(jnp.float32)[0:1, :]
    term = jnp.maximum(margin, 0.0) + jnp.log1p(jnp.exp(-jnp.abs(margin))) - label * margin
    total = term[:, 0:LANES]
    for h in range(1, term.shape[1] // LANES):
        total = total + term[:, h * LANES : (h + 1) * LANES]
    loss_ref[...] = total


def gradient_kernel(grains, glist, rlist, nb, resid, idt, vals_ref, out_ref, total):
    total[...] = jnp.zeros_like(total)
    group = lane_group()
    width = GROUP * GRAIN
    per = LANES // GRAIN

    def turn(t, carry):
        base = t * GROUP
        values = group_values(vals_ref, glist, base)
        offset = group_offsets(idt, rlist, base)
        parts = []
        for h in range(GROUP // per):
            row = jnp.zeros((1, LANES), jnp.float32)
            for i in range(per):
                row = jnp.where(group == i, resid[0, glist[base + h * per + i] // grains], row)
            parts.append(row)
        factor = jnp.broadcast_to(jnp.concatenate(parts, axis=1), (8, width))
        for c in range(total.shape[0] // CHUNK):
            spread = jnp.concatenate(
                [jnp.where(offset == c * CHUNK + i * 8, factor, 0.0) for i in range(CHUNK // 8)], axis=0
            ).astype(jnp.bfloat16)
            total[c * CHUNK : (c + 1) * CHUNK, :] += lax.dot_general(
                spread, values, NN, preferred_element_type=jnp.float32
            )
        return carry

    lax.fori_loop(0, nb[0], turn, jnp.int32(0))
    out_ref[...] = total[...].astype(jnp.bfloat16)


def scatter_kernel(n, grad_ref, margin_ref, owner_ref, loss_ref, sum_ref, notes_ref, notes, held, send, recv, nsend, nrecv):
    ex = margin_ref.shape[1]
    rows = sum_ref.shape[0]
    owner = owner_ref[...].astype(jnp.float32)
    square = jnp.broadcast_to(owner, (ex, ex))
    earlier = lax.broadcasted_iota(jnp.int32, (ex, ex), 0) < lax.broadcasted_iota(jnp.int32, (ex, ex), 1)
    same = jnp.where(jnp.logical_and(square.T == square, earlier), 1.0, 0.0)
    rank = jnp.sum(same, axis=0, keepdims=True)
    which = lax.broadcasted_iota(jnp.int32, (n, ex), 0).astype(jnp.float32)
    by_owner = jnp.where(which == owner, margin_ref[0:1, :], 0.0)
    place = lax.broadcasted_iota(jnp.int32, (LANES, ex), 0).astype(jnp.float32)
    by_rank = jnp.where(place == rank, 1.0, 0.0)
    ordered = lax.dot_general(
        by_owner, by_rank, NT, precision=lax.Precision.HIGHEST, preferred_element_type=jnp.float32
    )
    sub = lax.broadcasted_iota(jnp.int32, (8, LANES), 0)
    for d in range(n):
        notes[d] = jnp.where(sub == 0, ordered[d : d + 1, :], loss_ref[...])
    me = greet("rows", n)
    copies = []
    for k in range(1, n):
        peer = lax.rem(me + k, n)
        for source, target, out_sem, in_sem in (
            (grad_ref.at[pl.ds(pl.multiple_of(peer * rows, rows), rows)], held.at[k - 1], send, recv),
            (notes.at[peer], notes_ref.at[me], nsend, nrecv),
        ):
            copy = pltpu.make_async_remote_copy(
                src_ref=source,
                dst_ref=target,
                send_sem=out_sem.at[k - 1],
                recv_sem=in_sem.at[k - 1],
                device_id={"rows": peer},
                device_id_type=MESH,
            )
            copy.start()
            copies.append(copy)
    notes_ref[me] = notes[me]
    sum_ref[...] = grad_ref[pl.ds(pl.multiple_of(me * rows, rows), rows), :].astype(jnp.float32)
    for k in range(1, n):
        copies[2 * k - 2].wait()
        sum_ref[...] += held[k - 1].astype(jnp.float32)
        copies[2 * k - 1].wait()


def on_device(n, nf, tile_values, tile_blocks, tile_counts, labels, owner_rank, weights):
    ex, slots, width = tile_values.shape
    grains = slots // GRAIN
    rows = weights.shape[0]
    f32, i32, bf16 = jnp.float32, jnp.int32, jnp.bfloat16
    shape = jax.ShapeDtypeStruct
    dma = pltpu.SemaphoreType.DMA
    vals = tile_values.reshape(ex * grains, GRAIN, width)

    table = pl.pallas_call(
        functools.partial(gather_kernel, n),
        out_shape=shape((n * rows, width), bf16),
        in_specs=[VM],
        out_specs=VM,
        scratch_shapes=[pltpu.VMEM((rows, width), bf16), dma((n - 1,)), dma((n - 1,))],
        compiler_params=pltpu.CompilerParams(collective_id=0, has_side_effects=True),
    )(weights)

    listed = ex * grains + GROUP
    glist, rlist, nb, idt, partial = pl.pallas_call(
        margin_kernel,
        out_shape=(
            shape((listed,), i32),
            shape((listed,), i32),
            shape((1,), i32),
            shape((ex * grains + 8, LANES), i32),
            shape((8, ex), f32),
        ),
        in_specs=[SM, VM, VM, VM, VM],
        out_specs=(SM, SM, SM, VM, VM),
        scratch_shapes=[pltpu.VMEM((ex * grains + 8, LANES), f32)],
    )(tile_counts.reshape(ex), tile_counts, tile_blocks, table, vals)

    margin, resid, loss_part = pl.pallas_call(
        functools.partial(residual_kernel, nf),
        out_shape=(shape((8, ex), f32), shape((1, ex), f32), shape((8, LANES), f32)),
        in_specs=[VM, VM],
        out_specs=(VM, VM, VM),
        scratch_shapes=[pltpu.VMEM((nf, 8, ex), f32), dma((nf - 1,)), dma((nf - 1,))],
        compiler_params=pltpu.CompilerParams(collective_id=1, has_side_effects=True),
    )(partial, labels.reshape(1, ex))

    grad_part = pl.pallas_call(
        functools.partial(gradient_kernel, grains),
        out_shape=shape((n * rows, width), bf16),
        in_specs=[SM, SM, SM, SM, VM, VM],
        out_specs=VM,
        scratch_shapes=[pltpu.VMEM((n * rows, width), f32)],
    )(glist, rlist, nb, resid, idt, vals)

    gradient, notes = pl.pallas_call(
        functools.partial(scatter_kernel, n),
        out_shape=(shape((rows, width), f32), shape((n, 8, LANES), f32)),
        in_specs=[VM, VM, VM, VM],
        out_specs=(VM, VM),
        scratch_shapes=[
            pltpu.VMEM((n, 8, LANES), f32),
            pltpu.VMEM((n - 1, rows, width), bf16),
            dma((n - 1,)),
            dma((n - 1,)),
            dma((n - 1,)),
            dma((n - 1,)),
        ],
        compiler_params=pltpu.CompilerParams(collective_id=2, has_side_effects=True),
    )(grad_part, margin, owner_rank.reshape(1, ex), loss_part)

    owned_margins = notes[:, 0, : ex // n].reshape(ex)
    loss = jnp.sum(notes[:, 1, :]) / (ex * n)
    return owned_margins, gradient, loss


def solution(mesh):
    in_specs = (
        P("rows", "feat", None),
        P("rows", "feat"),
        P("rows", "feat"),
        P("rows"),
        P("rows"),
        P(("feat", "rows"), None),
    )
    out_specs = (P("rows"), P(("feat", "rows"), None), P())
    body = functools.partial(on_device, mesh.shape["rows"], mesh.shape["feat"])
    return jax.shard_map(body, mesh=mesh, in_specs=in_specs, out_specs=out_specs, check_vma=False)
```

time: 239 us -> 87.3 us (0.37)
  the two profiles are of different devices: /device:TPU:0 before, /device:TPU:11 now
where the time goes in v1:
time: 87.3 us; the launch traced here: 86.9 us
  Pallas kernels  77 us (88%)
  local copies, waits for them, and re-layouts  6.04 us (7%)
  between operations  2.45 us (3%)
  other arithmetic  1.37 us (2%)
    pallas_call x1, Pallas kernels, on_device(): pl.pallas_call(functools.partial(scatter_kernel, n), out_shape=(shape((ro...  23.5 us
    pallas_call x1, Pallas kernels, on_device(): pl.pallas_call(functools.partial(gather_kernel, n), out_shape=shape((n *...  17.7 us
    pallas_call x1, Pallas kernels, on_device(): pl.pallas_call(margin_kernel, out_shape=(shape((listed,), i32), shape((li...  16.5 us
    pallas_call x1, Pallas kernels, on_device(): pl.pallas_call(functools.partial(gradient_kernel, grains), out_shape=shap...  14 us
    pallas_call x1, Pallas kernels, on_device(): pl.pallas_call(functools.partial(residual_kernel, nf), out_shape=(shape((...  5.19 us
    unnamed x3, local copies, waits for them, and re-layouts  4.63 us

profile of v1, /device:TPU:11, one launch (start us, length us, event | category | flops | bytes accessed | tf_op | source)
XLA Modules:
  0.0 86.9 jit_solution(1061208872661171532)
XLA Ops:
  0.6 1.6 %copy.10.ids_ref = s32[256,64]{1,0:T(8,128)} copy(s32[256,64]{0,1:T(8,128)} %param.7) | data formatting | bytes 131072 | tf_op args[1]
  2.2 1.5 %copy.9.used_ref = s32[256,1]{1,0:T(8,128)} copy(s32[256,1]{0,1:T(1,128)} %param.8) | data formatting | bytes 2048 | tf_op args[2]
  3.7 17.7 %shard_map.85.table_ref = bf16[2048,128]{1,0:T(8,128)(2,1)} custom-call(f32[256,128]{1,0:T(8,128)} %w_ref.1), custom_call_target="tpu_custom_call" | custom-call | tf_op jit(solution)/shard_map/pallas_call | solution.py:248
  21.4 16.5 %shard_map.86 = (s32[1040]{0:T(1024)}, s32[1040]{0:T(1024)}, s32[1]{0:T(128)}, s32[1032,128]{1,0:T(8,128)}, f32[8,256]{1,0:T(8,128)}) custom-call(s32[256]{0:T(256)} %bitcast.6, s32[256,1]{1,0:T(8,128)} %copy.9.used_ref, s32[256,64]{1,0:T(8,128)} %copy.10.ids_ref, bf16[2048,128]{1,0:T(8,128)(2,1)} %shard_map.85.table_ref, bf16[1024,16,128]{2,1,0:T(8,128)(2,1)} %bitcast.4), custom_call_target="tpu_custom_call" | custom-call | tf_op jit(solution)/shard_map/pallas_call | solution.py:258
  37.9 5.2 %shard_map.87 = (f32[8,256]{1,0:T(8,128)}, f32[1,256]{1,0:T(1,128)}, f32[8,128]{1,0:T(8,128)}) custom-call(f32[8,256]{1,0:T(8,128)} %get-tuple-element.16.partial_ref, s32[1,256]{1,0:T(1,128)} %bitcast.8), custom_call_target="tpu_custom_call" | custom-call | tf_op jit(solution)/shard_map/pallas_call | solution.py:272
  43.1 14.0 %shard_map.88.grad_ref = bf16[2048,128]{1,0:T(8,128)(2,1)} custom-call(s32[1040]{0:T(1024)} %get-tuple-element.13.glist, s32[1040]{0:T(1024)} %get-tuple-element.14.rlist, s32[1]{0:T(128)} %get-tuple-element.15.nb, f32[1,256]{1,0:T(1,128)} %get-tuple-element.17.resid, s32[1032,128]{1,0:T(8,128)} %get-tuple-element.18.idt, bf16[1024,16,128]{2,1,0:T(8,128)(2,1)} %bitcast.5), custom_call_target="tpu_custom_call" | custom-call | tf_op jit(solution)/shard_map/pallas_call | solution.py:281
  57.2 23.5 %shard_map.89 = (f32[256,128]{1,0:T(8,128)}, f32[8,8,128]{2,1,0:T(8,128)}) custom-call(bf16[2048,128]{1,0:T(8,128)(2,1)} %shard_map.88.grad_ref, f32[8,256]{1,0:T(8,128)} %get-tuple-element.19.margin_ref, s32[1,256]{1,0:T(1,128)} %bitcast.7, f32[8,128]{1,0:T(8,128)} %get-tuple-element.20.loss_ref), custom_call_target="tpu_custom_call" | custom-call | tf_op jit(solution)/shard_map/pallas_call | solution.py:289
  80.7 1.4 %slice_reduce_fusion = f32[]{:T(128)} fusion(f32[8,8,128]{2,1,0:T(8,128)} %get-tuple-element.21), kind=kLoop, calls=%fused_computation | loop fusion | flops 1023 | bytes 4100 | tf_op jit(solution)/shard_map/reduce_sum | solution.py:306
  82.7 0.8 slice_reduce_fusion.1
  83.5 0.6 reshape_squeeze.3
  84.2 1.6 %copy.12 = f32[256,128]{1,0:T(8,128)} copy(f32[256,128]{1,0:T(8,128)} %get-tuple-element.27) | data formatting | bytes 262144

commit v2 on v1

--- a/solution.py
+++ b/solution.py
@@ -11,6 +11,8 @@
 LANES = 128
 GRAIN = 16
 GROUP = 16
+GRANT = 24 * 1024 * 1024
+COST = pl.CostEstimate(flops=0, bytes_accessed=24 * 1024 * 1024, transcendentals=0)
 CHUNK = 256
 NT = (((1,), (1,)), ((), ()))
 NN = (((1,), (0,)), ((), ()))
@@ -18,35 +20,53 @@
 SM = pl.BlockSpec(memory_space=pltpu.SMEM)
 
 
-def greet(axis, count):
-    me = lax.axis_index(axis)
+def seat(n):
+    me = lax.axis_index("rows")
+    side = lax.rem(me, 2)
+    partner = me + 1 - 2 * side
+    column = [lax.rem(me + 2 * k, n) for k in range(n // 2)]
+    source = [lax.rem(me + n - 2 * k, n) for k in range(n // 2)]
+    return me, partner, column, source
+
+
+def greet(axis, peers):
     barrier = pltpu.get_barrier_semaphore()
-    for k in range(1, count):
-        peer = lax.rem(me + k, count)
+    for peer in peers:
         pl.semaphore_signal(barrier, inc=1, device_id={axis: peer}, device_id_type=MESH)
-    pl.semaphore_wait(barrier, count - 1)
-    return me
-
-
-def gather_kernel(n, w_ref, table_ref, half, send, recv):
-    rows = w_ref.shape[0]
+    pl.semaphore_wait(barrier, len(peers))
+
+
+def send_to(axis, peer, source, target, send, recv):
+    copy = pltpu.make_async_remote_copy(
+        src_ref=source,
+        dst_ref=target,
+        send_sem=send,
+        recv_sem=recv,
+        device_id={axis: peer},
+        device_id_type=MESH,
+    )
+    copy.start()
+    return copy
+
+
+def gather_kernel(n, w_ref, table_ref, half, send, recv, xsend, xrecv):
     half[...] = w_ref[...].astype(jnp.bfloat16)
-    me = greet("rows", n)
-    here = pl.ds(pl.multiple_of(me * rows, rows), rows)
-    copies = []
-    for k in range(1, n):
-        copy = pltpu.make_async_remote_copy(
-            src_ref=half,
-            dst_ref=table_ref.at[here],
-            send_sem=send.at[k - 1],
-            recv_sem=recv.at[k - 1],
-            device_id={"rows": lax.rem(me + k, n)},
-            device_id_type=MESH,
-        )
-        copy.start()
-        copies.append(copy)
-    table_ref[here, :] = w_ref[...].astype(jnp.bfloat16)
-    for copy in copies:
+    me, partner, column, source = seat(n)
+    deep = n // 2
+    greet("rows", [partner] + column[1:])
+    across = [send_to("rows", partner, half, table_ref.at[me], xsend.at[0], xrecv.at[0])]
+    along = [
+        send_to("rows", column[k], half, table_ref.at[me], send.at[k - 1], recv.at[k - 1])
+        for k in range(1, deep)
+    ]
+    table_ref[me] = w_ref[...].astype(jnp.bfloat16)
+    for k in range(1, deep):
+        along[k - 1].wait_recv()
+        block = table_ref.at[source[k]]
+        across.append(send_to("rows", partner, block, block, xsend.at[k], xrecv.at[k]))
+    for copy in along:
+        copy.wait_send()
+    for copy in across:
         copy.wait()
 
 
@@ -73,12 +93,13 @@
 
 
 def margin_kernel(counts, used_ref, ids_ref, table_ref, vals_ref, glist, rlist, nb, idt, partial_ref, terms):
-    ex, slots = ids_ref.shape
+    slots, ex = ids_ref.shape
     grains = slots // GRAIN
-    live = lax.broadcasted_iota(jnp.int32, (ex, slots), 1) < used_ref[...]
+    live = lax.broadcasted_iota(jnp.int32, (slots, ex), 0) < used_ref[...]
     shifted = jnp.where(live, ids_ref[...] + 1, 0)
     if slots < LANES:
-        shifted = jnp.concatenate([shifted, jnp.zeros((ex, LANES - slots), jnp.int32)], axis=1)
+        shifted = jnp.concatenate([shifted, jnp.zeros((LANES - slots, ex), jnp.int32)], axis=0)
+    shifted = shifted.T
     lane = lax.broadcasted_iota(jnp.int32, (ex, LANES), 1) // GRAIN
     for q in range(grains):
         piece = jnp.where(lane == q, shifted, 0)
@@ -132,19 +153,13 @@
 
 
 def residual_kernel(n, partial_ref, labels_ref, margin_ref, resid_ref, loss_ref, held, send, recv):
-    me = greet("feat", n)
-    copies = []
-    for k in range(1, n):
-        copy = pltpu.make_async_remote_copy(
-            src_ref=partial_ref,
-            dst_ref=held.at[me],
-            send_sem=send.at[k - 1],
-            recv_sem=recv.at[k - 1],
-            device_id={"feat": lax.rem(me + k, n)},
-            device_id_type=MESH,
-        )
-        copy.start()
-        copies.append(copy)
+    me = lax.axis_index("feat")
+    peers = [lax.rem(me + k, n) for k in range(1, n)]
+    greet("feat", peers)
+    copies = [
+        send_to("feat", peer, partial_ref, held.at[me], send.at[k], recv.at[k])
+        for k, peer in enumerate(peers)
+    ]
     held[me] = partial_ref[...]
     for copy in copies:
         copy.wait()
@@ -192,9 +207,8 @@
     out_ref[...] = total[...].astype(jnp.bfloat16)
 
 
-def scatter_kernel(n, grad_ref, margin_ref, owner_ref, loss_ref, sum_ref, notes_ref, notes, held, send, recv, nsend, nrecv):
+def scatter_kernel(n, grad_ref, margin_ref, owner_ref, loss_ref, sum_ref, notes_ref, notes, crossed, paired, held, send, recv, xsend, xrecv, nsend, nrecv):
     ex = margin_ref.shape[1]
-    rows = sum_ref.shape[0]
     owner = owner_ref[...].astype(jnp.float32)
     square = jnp.broadcast_to(owner, (ex, ex))
     earlier = lax.broadcasted_iota(jnp.int32, (ex, ex), 0) < lax.broadcasted_iota(jnp.int32, (ex, ex), 1)
@@ -210,36 +224,48 @@
     sub = lax.broadcasted_iota(jnp.int32, (8, LANES), 0)
     for d in range(n):
         notes[d] = jnp.where(sub == 0, ordered[d : d + 1, :], loss_ref[...])
-    me = greet("rows", n)
-    copies = []
-    for k in range(1, n):
-        peer = lax.rem(me + k, n)
-        for source, target, out_sem, in_sem in (
-            (grad_ref.at[pl.ds(pl.multiple_of(peer * rows, rows), rows)], held.at[k - 1], send, recv),
-            (notes.at[peer], notes_ref.at[me], nsend, nrecv),
-        ):
-            copy = pltpu.make_async_remote_copy(
-                src_ref=source,
-                dst_ref=target,
-                send_sem=out_sem.at[k - 1],
-                recv_sem=in_sem.at[k - 1],
-                device_id={"rows": peer},
-                device_id_type=MESH,
-            )
-            copy.start()
-            copies.append(copy)
+    me, partner, column, source = seat(n)
+    side = me - partner
+    deep = n // 2
+    others = [lax.rem(me + k, n) for k in range(1, n)]
+    greet("rows", others)
+    order = list(range(1, deep)) + [0]
+    across = {
+        k: send_to("rows", partner, grad_ref.at[column[k] - side], crossed.at[k], xsend.at[k], xrecv.at[k])
+        for k in order
+    }
+    told = [
+        send_to("rows", peer, notes.at[peer], notes_ref.at[me], nsend.at[k], nrecv.at[k])
+        for k, peer in enumerate(others)
+    ]
     notes_ref[me] = notes[me]
-    sum_ref[...] = grad_ref[pl.ds(pl.multiple_of(me * rows, rows), rows), :].astype(jnp.float32)
-    for k in range(1, n):
-        copies[2 * k - 2].wait()
-        sum_ref[...] += held[k - 1].astype(jnp.float32)
-        copies[2 * k - 1].wait()
+    along = []
+    for k in range(1, deep):
+        across[k].wait_recv()
+        pair = grad_ref[column[k]].astype(jnp.float32) + crossed[k].astype(jnp.float32)
+        paired[k - 1] = pair.astype(jnp.bfloat16)
+        along.append(
+            send_to("rows", column[k], paired.at[k - 1], held.at[k - 1], send.at[k - 1], recv.at[k - 1])
+        )
+    across[0].wait_recv()
+    total = grad_ref[me].astype(jnp.float32) + crossed[0].astype(jnp.float32)
+    for k in range(1, deep):
+        along[k - 1].wait_recv()
+        total = total + held[k - 1].astype(jnp.float32)
+    sum_ref[...] = total
+    for k in order:
+        across[k].wait_send()
+    for copy in along:
+        copy.wait_send()
+    for copy in told:
+        copy.wait()
 
 
 def on_device(n, nf, tile_values, tile_blocks, tile_counts, labels, owner_rank, weights):
     ex, slots, width = tile_values.shape
     grains = slots // GRAIN
     rows = weights.shape[0]
+    deep = n // 2
     f32, i32, bf16 = jnp.float32, jnp.int32, jnp.bfloat16
     shape = jax.ShapeDtypeStruct
     dma = pltpu.SemaphoreType.DMA
@@ -247,12 +273,13 @@
 
     table = pl.pallas_call(
         functools.partial(gather_kernel, n),
-        out_shape=shape((n * rows, width), bf16),
+        out_shape=shape((n, rows, width), bf16),
         in_specs=[VM],
         out_specs=VM,
-        scratch_shapes=[pltpu.VMEM((rows, width), bf16), dma((n - 1,)), dma((n - 1,))],
-        compiler_params=pltpu.CompilerParams(collective_id=0, has_side_effects=True),
-    )(weights)
+        scratch_shapes=[pltpu.VMEM((rows, width), bf16), dma((deep - 1,)), dma((deep - 1,)), dma((deep,)), dma((deep,))],
+        compiler_params=pltpu.CompilerParams(collective_id=0, has_side_effects=True, vmem_limit_bytes=GRANT),
+        cost_estimate=COST,
+    )(weights).reshape(n * rows, width)
 
     listed = ex * grains + GROUP
     glist, rlist, nb, idt, partial = pl.pallas_call(
@@ -267,7 +294,9 @@
         in_specs=[SM, VM, VM, VM, VM],
         out_specs=(SM, SM, SM, VM, VM),
         scratch_shapes=[pltpu.VMEM((ex * grains + 8, LANES), f32)],
-    )(tile_counts.reshape(ex), tile_counts, tile_blocks, table, vals)
+        compiler_params=pltpu.CompilerParams(vmem_limit_bytes=GRANT),
+        cost_estimate=COST,
+    )(tile_counts.reshape(ex), tile_counts.reshape(1, ex), tile_blocks.T, table, vals)
 
     margin, resid, loss_part = pl.pallas_call(
         functools.partial(residual_kernel, nf),
@@ -275,7 +304,8 @@
         in_specs=[VM, VM],
         out_specs=(VM, VM, VM),
         scratch_shapes=[pltpu.VMEM((nf, 8, ex), f32), dma((nf - 1,)), dma((nf - 1,))],
-        compiler_params=pltpu.CompilerParams(collective_id=1, has_side_effects=True),
+        compiler_params=pltpu.CompilerParams(collective_id=1, has_side_effects=True, vmem_limit_bytes=GRANT),
+        cost_estimate=COST,
     )(partial, labels.reshape(1, ex))
 
     grad_part = pl.pallas_call(
@@ -284,6 +314,8 @@
         in_specs=[SM, SM, SM, SM, VM, VM],
         out_specs=VM,
         scratch_shapes=[pltpu.VMEM((n * rows, width), f32)],
+        compiler_params=pltpu.CompilerParams(vmem_limit_bytes=GRANT),
+        cost_estimate=COST,
     )(glist, rlist, nb, resid, idt, vals)
 
     gradient, notes = pl.pallas_call(
@@ -293,14 +325,19 @@
         out_specs=(VM, VM),
         scratch_shapes=[
             pltpu.VMEM((n, 8, LANES), f32),
-            pltpu.VMEM((n - 1, rows, width), bf16),
-            dma((n - 1,)),
-            dma((n - 1,)),
+            pltpu.VMEM((deep, rows, width), bf16),
+            pltpu.VMEM((deep - 1, rows, width), bf16),
+            pltpu.VMEM((deep - 1, rows, width), bf16),
+            dma((deep - 1,)),
+            dma((deep - 1,)),
+            dma((deep,)),
+            dma((deep,)),
             dma((n - 1,)),
             dma((n - 1,)),
         ],
-        compiler_params=pltpu.CompilerParams(collective_id=2, has_side_effects=True),
-    )(grad_part, margin, owner_rank.reshape(1, ex), loss_part)
+        compiler_params=pltpu.CompilerParams(collective_id=2, has_side_effects=True, vmem_limit_bytes=GRANT),
+        cost_estimate=COST,
+    )(grad_part.reshape(n, rows, width), margin, owner_rank.reshape(1, ex), loss_part)
 
     owned_margins = notes[:, 0, : ex // n].reshape(ex)
     loss = jnp.sum(notes[:, 1, :]) / (ex * n)

time: 87.3 us -> 73 us (0.84)
  the two profiles are of different devices: /device:TPU:11 before, /device:TPU:0 now
where the time goes in v2:
time: 73 us; the launch traced here: 72.9 us
  Pallas kernels  63.8 us (87%)
  local copies, waits for them, and re-layouts  5.93 us (8%)
  between operations  2.51 us (3%)
    pallas_call x1, Pallas kernels, on_device(): pl.pallas_call(functools.partial(scatter_kernel, n), out_shape=(shape((ro...  20.4 us
    pallas_call x1, Pallas kernels, on_device(): pl.pallas_call(functools.partial(gather_kernel, n), out_shape=shape((n, r...  15.6 us
    pallas_call x1, Pallas kernels, on_device(): pl.pallas_call(margin_kernel, out_shape=(shape((listed,), i32), shape((li...  13.6 us
    pallas_call x1, Pallas kernels, on_device(): pl.pallas_call(functools.partial(gradient_kernel, grains), out_shape=shap...  10.6 us
    unnamed x15, local copies, waits for them, and re-layouts  5.27 us
    pallas_call x1, Pallas kernels, on_device(): pl.pallas_call(functools.partial(residual_kernel, nf), out_shape=(shape((...  3.78 us

profile of v2, /device:TPU:0, one launch (start us, length us, event | category | flops | bytes accessed | tf_op | source)
XLA Modules:
  0.0 72.9 jit_solution(15437088671455608231)
XLA Ops:
  0.6 0.0 copy-start.6
  0.6 0.0 copy-start.2
  0.7 0.9 %copy-done.2 = f32[256,128]{1,0:T(8,128)S(1)} copy-done((f32[256,128]{1,0:T(8,128)S(1)}, f32[256,128]{1,0:T(8,128)}, u32[]{:S(2)}) %copy-start.2) | copy-done | bytes 131096
  1.6 15.6 %shard_map.85 = bf16[8,256,128]{2,1,0:T(8,128)(2,1)S(1)} custom-call(f32[256,128]{1,0:T(8,128)S(1)} %copy-done.2), custom_call_target="tpu_custom_call" | custom-call | bytes 25165824 | tf_op jit(solution)/shard_map/pallas_call | solution.py:274
  17.1 0.0 copy-start
  17.1 2.2 %copy-done = bf16[256,64,128]{2,1,0:T(8,128)(2,1)S(1)} copy-done((bf16[256,64,128]{2,1,0:T(8,128)(2,1)S(1)}, bf16[256,64,128]{2,1,0:T(8,128)(2,1)}, u32[]{:S(2)}) %copy-start) | copy-done | bytes 4194328
  19.3 0.0 copy-start.3
  19.3 0.8 %copy-done.3 = s32[256,64]{0,1:T(8,128)S(1)} copy-done((s32[256,64]{0,1:T(8,128)S(1)}, s32[256,64]{0,1:T(8,128)}, u32[]{:S(2)}) %copy-start.3) | copy-done | bytes 65560
  20.1 0.0 copy-start.4
  20.1 0.7 copy-done.4
  20.8 0.0 copy-start.1
  20.8 0.0 copy-start.5
  20.8 13.6 %shard_map.86 = (s32[1040]{0:T(1024)S(1)}, s32[1040]{0:T(1024)S(1)}, s32[1]{0:T(128)}, s32[1032,128]{1,0:T(8,128)S(1)}, f32[8,256]{1,0:T(8,128)S(1)}) custom-call(s32[256]{0:T(256)S(1)} %bitcast.13, s32[1,256]{1,0:T(1,128)S(1)} %bitcast.14, s32[64,256]{1,0:T(8,128)S(1)} %bitcast.12, bf16[2048,128]{1,0:T(8,128)(2,1)S(1)} %bitcast.10, ...), custom_call_target="tpu_custom_call" | custom-call | bytes 25165824 | tf_op jit(solution)/shard_map/pallas_call | solution.py:285
  34.4 0.0 copy-done.6
  34.4 3.8 %shard_map.87 = (f32[8,256]{1,0:T(8,128)S(1)}, f32[1,256]{1,0:T(1,128)S(1)}, f32[8,128]{1,0:T(8,128)S(1)}) custom-call(f32[8,256]{1,0:T(8,128)S(1)} %get-tuple-element.16.partial_ref, s32[1,256]{1,0:T(1,128)S(1)} %bitcast.16), custom_call_target="tpu_custom_call" | custom-call | bytes 25165824 | tf_op jit(solution)/shard_map/pallas_call | solution.py:301
  38.2 0.0 copy-done.1
  38.2 10.6 %shard_map.88 = bf16[2048,128]{1,0:T(8,128)(2,1)S(1)} custom-call(s32[1040]{0:T(1024)S(1)} %get-tuple-element.13.glist, s32[1040]{0:T(1024)S(1)} %get-tuple-element.14.rlist, s32[1]{0:T(128)} %get-tuple-element.15.nb, f32[1,256]{1,0:T(1,128)S(1)} %get-tuple-element.17.resid, s32[1032,128]{1,0:T(8,128)S(1)} %get-tuple-element.18.idt, ...), custom_call_target="tpu_custom_call" | custom-call | bytes 25165824 | tf_op jit(solution)/shard_map/pallas_call | solution.py:311
  48.8 0.0 copy-done.5
  48.8 20.4 %shard_map.89 = (f32[256,128]{1,0:T(8,128)S(1)}, f32[8,8,128]{2,1,0:T(8,128)S(1)}) custom-call(bf16[8,256,128]{2,1,0:T(8,128)(2,1)S(1)} %bitcast.11, f32[8,256]{1,0:T(8,128)S(1)} %get-tuple-element.19.margin_ref, s32[1,256]{1,0:T(1,128)S(1)} %bitcast.15, f32[8,128]{1,0:T(8,128)S(1)} %get-tuple-element.20.loss_ref), custom_call_target="tpu_custom_call" | custom-call | bytes 25165824 | tf_op jit(solution)/shard_map/pallas_call | solution.py:321
  69.2 0.6 slice_reduce_fusion
  70.4 0.6 reshape_squeeze.3
  71.1 0.7 copy.10
  (1 shorter events, 0.0 us)
Async XLA Ops:
  0.6 33.8 %copy-start.6 = (s32[256]{0:T(256)S(1)}, s32[256]{0:T(256)}, u32[]{:S(2)}) copy-start(s32[256]{0:T(256)} %param.9) | copy-start | bytes 3076
  0.6 0.9 %copy-start.2 = (f32[256,128]{1,0:T(8,128)S(1)}, f32[256,128]{1,0:T(8,128)}, u32[]{:S(2)}) copy-start(f32[256,128]{1,0:T(8,128)} %w_ref.1) | copy-start | bytes 393220
  17.1 2.2 %copy-start = (bf16[256,64,128]{2,1,0:T(8,128)(2,1)S(1)}, bf16[256,64,128]{2,1,0:T(8,128)(2,1)}, u32[]{:S(2)}) copy-start(bf16[256,64,128]{2,1,0:T(8,128)(2,1)} %param.6) | copy-start | bytes 12582916
  19.3 0.8 %copy-start.3 = (s32[256,64]{0,1:T(8,128)S(1)}, s32[256,64]{0,1:T(8,128)}, u32[]{:S(2)}) copy-start(s32[256,64]{0,1:T(8,128)} %param.7) | copy-start | bytes 196612
  20.1 0.7 copy-start.4
  20.8 17.4 %copy-start.1 = (bf16[256,64,128]{2,1,0:T(8,128)(2,1)S(1)}, bf16[256,64,128]{2,1,0:T(8,128)(2,1)}, u32[]{:S(2)}) copy-start(bf16[256,64,128]{2,1,0:T(8,128)(2,1)} %param.6) | copy-start | bytes 12582916
  20.8 28.0 %copy-start.5 = (s32[256]{0:T(256)S(1)}, s32[256]{0:T(256)}, u32[]{:S(2)}) copy-start(s32[256]{0:T(256)} %param.10) | copy-start | bytes 3076

commit v3 on v2

--- a/solution.py
+++ b/solution.py
@@ -9,8 +9,8 @@
 
 MESH = pl.DeviceIdType.MESH
 LANES = 128
-GRAIN = 16
-GROUP = 16
+GRAIN = 8
+GROUP = 32
 GRANT = 24 * 1024 * 1024
 COST = pl.CostEstimate(flops=0, bytes_accessed=24 * 1024 * 1024, transcendentals=0)
 CHUNK = 256
@@ -49,7 +49,7 @@
     return copy
 
 
-def gather_kernel(n, w_ref, table_ref, half, send, recv, xsend, xrecv):
+def gather_kernel(n, w_ref, vals_in, ids_in, used_in, table_ref, vals_ref, ids_ref, used_ref, half, send, recv, xsend, xrecv, lsem):
     half[...] = w_ref[...].astype(jnp.bfloat16)
     me, partner, column, source = seat(n)
     deep = n // 2
@@ -59,6 +59,14 @@
         send_to("rows", column[k], half, table_ref.at[me], send.at[k - 1], recv.at[k - 1])
         for k in range(1, deep)
     ]
+    brought = [
+        pltpu.make_async_copy(source_ref, target_ref, lsem.at[k])
+        for k, (source_ref, target_ref) in enumerate(
+            ((ids_in, ids_ref), (used_in, used_ref), (vals_in, vals_ref))
+        )
+    ]
+    for copy in brought:
+        copy.start()
     table_ref[me] = w_ref[...].astype(jnp.bfloat16)
     for k in range(1, deep):
         along[k - 1].wait_recv()
@@ -66,7 +74,7 @@
         across.append(send_to("rows", partner, block, block, xsend.at[k], xrecv.at[k]))
     for copy in along:
         copy.wait_send()
-    for copy in across:
+    for copy in across + brought:
         copy.wait()
 
 
@@ -271,15 +279,29 @@
     dma = pltpu.SemaphoreType.DMA
     vals = tile_values.reshape(ex * grains, GRAIN, width)
 
-    table = pl.pallas_call(
+    ANY = pl.BlockSpec(memory_space=pltpu.MemorySpace.HBM)
+    table, vals, ids, used = pl.pallas_call(
         functools.partial(gather_kernel, n),
-        out_shape=shape((n, rows, width), bf16),
-        in_specs=[VM],
-        out_specs=VM,
-        scratch_shapes=[pltpu.VMEM((rows, width), bf16), dma((deep - 1,)), dma((deep - 1,)), dma((deep,)), dma((deep,))],
+        out_shape=(
+            shape((n, rows, width), bf16),
+            shape(vals.shape, bf16),
+            shape((slots, ex), i32),
+            shape((1, ex), i32),
+        ),
+        in_specs=[VM, ANY, ANY, ANY],
+        out_specs=(VM, VM, VM, VM),
+        scratch_shapes=[
+            pltpu.VMEM((rows, width), bf16),
+            dma((deep - 1,)),
+            dma((deep - 1,)),
+            dma((deep,)),
+            dma((deep,)),
+            dma((3,)),
+        ],
         compiler_params=pltpu.CompilerParams(collective_id=0, has_side_effects=True, vmem_limit_bytes=GRANT),
         cost_estimate=COST,
-    )(weights).reshape(n * rows, width)
+    )(weights, vals, tile_blocks.T, tile_counts.reshape(1, ex))
+    table = table.reshape(n * rows, width)
 
     listed = ex * grains + GROUP
     glist, rlist, nb, idt, partial = pl.pallas_call(
@@ -296,7 +318,7 @@
         scratch_shapes=[pltpu.VMEM((ex * grains + 8, LANES), f32)],
         compiler_params=pltpu.CompilerParams(vmem_limit_bytes=GRANT),
         cost_estimate=COST,
-    )(tile_counts.reshape(ex), tile_counts.reshape(1, ex), tile_blocks.T, table, vals)
+    )(used.reshape(ex), used, ids, table, vals)
 
     margin, resid, loss_part = pl.pallas_call(
         functools.partial(residual_kernel, nf),

time: 73 us -> 73.4 us (level)
    pallas_call x1, Pallas kernels: 20.4 us -> 22.8 us  [on_device(): pl.pallas_call(functools.partial(scatter_kernel, n), out_shape=(shape((ro...]
    pallas_call x1, Pallas kernels: 10.6 us -> 8.21 us  [on_device(): pl.pallas_call(functools.partial(gradient_kernel, grains), out_shape=shap...]
    unnamed x15 -> x13, local copies, waits for them, and re-layouts: 5.27 us -> 5.27 us
where the time goes in v3:
time: 73.4 us; the launch traced here: 73.1 us
  Pallas kernels  64.1 us (87%)
  local copies, waits for them, and re-layouts  5.92 us (8%)
  between operations  2.5 us (3%)
    pallas_call x1, Pallas kernels, on_device(): pl.pallas_call(functools.partial(scatter_kernel, n), out_shape=(shape((ro...  22.8 us
    pallas_call x1, Pallas kernels, on_device(): pl.pallas_call(functools.partial(gather_kernel, n), out_shape=(shape((n,...  15.6 us
    pallas_call x1, Pallas kernels, on_device(): pl.pallas_call(margin_kernel, out_shape=(shape((listed,), i32), shape((li...  13.7 us
    pallas_call x1, Pallas kernels, on_device(): pl.pallas_call(functools.partial(gradient_kernel, grains), out_shape=shap...  8.21 us
    unnamed x13, local copies, waits for them, and re-layouts  5.27 us
    pallas_call x1, Pallas kernels, on_device(): pl.pallas_call(functools.partial(residual_kernel, nf), out_shape=(shape((...  3.78 us

profile of v3, /device:TPU:0, one launch (start us, length us, event | category | flops | bytes accessed | tf_op | source)
XLA Modules:
  0.0 73.1 jit_solution(4364003522523367264)
XLA Ops:
  0.6 0.0 copy-start
  0.6 2.2 %copy-done = bf16[256,64,128]{2,1,0:T(8,128)(2,1)S(1)} copy-done((bf16[256,64,128]{2,1,0:T(8,128)(2,1)S(1)}, bf16[256,64,128]{2,1,0:T(8,128)(2,1)}, u32[]{:S(2)}) %copy-start) | copy-done | bytes 4194328
  2.8 0.0 copy-start.1
  2.8 0.9 %copy-done.1 = f32[256,128]{1,0:T(8,128)S(1)} copy-done((f32[256,128]{1,0:T(8,128)S(1)}, f32[256,128]{1,0:T(8,128)}, u32[]{:S(2)}) %copy-start.1) | copy-done | bytes 131096
  3.7 0.0 copy-start.2
  3.7 0.8 %copy-done.2 = s32[256,64]{0,1:T(8,128)S(1)} copy-done((s32[256,64]{0,1:T(8,128)S(1)}, s32[256,64]{0,1:T(8,128)}, u32[]{:S(2)}) %copy-start.2) | copy-done | bytes 65560
  4.6 0.0 copy-start.3
  4.6 0.7 copy-done.3
  5.2 0.0 copy-start.5
  5.2 15.6 %shard_map.85 = (bf16[8,256,128]{2,1,0:T(8,128)(2,1)S(1)}, bf16[2048,8,128]{2,1,0:T(8,128)(2,1)S(1)}, s32[64,256]{1,0:T(8,128)S(1)}, s32[1,256]{1,0:T(1,128)S(1)}) custom-call(f32[256,128]{1,0:T(8,128)S(1)} %copy-done.1, bf16[2048,8,128]{2,1,0:T(8,128)(2,1)S(1)} %bitcast.8, s32[64,256]{1,0:T(8,128)S(1)} %bitcast.11, s32[1,256]{1,0:T(1,128)S(1)} %bitcast.13), custom_call_target="tpu_custom_call" | custom-call | bytes 25165824 | tf_op jit(solution)/shard_map/pallas_call | solution.py:283
  20.8 0.0 copy-start.4
  20.9 13.7 %shard_map.86 = (s32[2080]{0:T(1024)S(1)}, s32[2080]{0:T(1024)S(1)}, s32[1]{0:T(128)}, s32[2056,128]{1,0:T(8,128)S(1)}, f32[8,256]{1,0:T(8,128)S(1)}) custom-call(s32[256]{0:T(256)S(1)} %bitcast.12, s32[1,256]{1,0:T(1,128)S(1)} %get-tuple-element.17.used_ref, s32[64,256]{1,0:T(8,128)S(1)} %get-tuple-element.18.ids_ref, bf16[2048,128]{1,0:T(8,128)(2,1)S(1)} %bitcast.10, ...), custom_call_target="tpu_custom_call" | custom-call | bytes 25165824 | tf_op jit(solution)/shard_map/pallas_call | solution.py:307
  34.6 0.0 copy-done.5
  34.6 3.8 %shard_map.87 = (f32[8,256]{1,0:T(8,128)S(1)}, f32[1,256]{1,0:T(1,128)S(1)}, f32[8,128]{1,0:T(8,128)S(1)}) custom-call(f32[8,256]{1,0:T(8,128)S(1)} %get-tuple-element.24.partial_ref, s32[1,256]{1,0:T(1,128)S(1)} %bitcast.15), custom_call_target="tpu_custom_call" | custom-call | bytes 25165824 | tf_op jit(solution)/shard_map/pallas_call | solution.py:323
  38.4 8.2 %shard_map.88 = bf16[2048,128]{1,0:T(8,128)(2,1)S(1)} custom-call(s32[2080]{0:T(1024)S(1)} %get-tuple-element.21.glist, s32[2080]{0:T(1024)S(1)} %get-tuple-element.22.rlist, s32[1]{0:T(128)} %get-tuple-element.23.nb, f32[1,256]{1,0:T(1,128)S(1)} %get-tuple-element.25.resid, s32[2056,128]{1,0:T(8,128)S(1)} %get-tuple-element.26.idt, ...), custom_call_target="tpu_custom_call" | custom-call | bytes 25165824 | tf_op jit(solution)/shard_map/pallas_call | solution.py:333
  46.6 0.0 copy-done.4
  46.6 22.8 %shard_map.89 = (f32[256,128]{1,0:T(8,128)S(1)}, f32[8,8,128]{2,1,0:T(8,128)S(1)}) custom-call(bf16[8,256,128]{2,1,0:T(8,128)(2,1)S(1)} %bitcast.9, f32[8,256]{1,0:T(8,128)S(1)} %get-tuple-element.27.margin_ref, s32[1,256]{1,0:T(1,128)S(1)} %bitcast.14, f32[8,128]{1,0:T(8,128)S(1)} %get-tuple-element.28.loss_ref), custom_call_target="tpu_custom_call" | custom-call | bytes 25165824 | tf_op jit(solution)/shard_map/pallas_call | solution.py:343
  69.4 0.6 slice_reduce_fusion
  70.7 0.6 reshape_squeeze.3
  71.3 0.7 copy.10
  (1 shorter events, 0.0 us)
Async XLA Ops:
  0.6 2.2 %copy-start = (bf16[256,64,128]{2,1,0:T(8,128)(2,1)S(1)}, bf16[256,64,128]{2,1,0:T(8,128)(2,1)}, u32[]{:S(2)}) copy-start(bf16[256,64,128]{2,1,0:T(8,128)(2,1)} %param.6) | copy-start | bytes 12582916
  2.8 0.9 %copy-start.1 = (f32[256,128]{1,0:T(8,128)S(1)}, f32[256,128]{1,0:T(8,128)}, u32[]{:S(2)}) copy-start(f32[256,128]{1,0:T(8,128)} %w_ref.1) | copy-start | bytes 393220
  3.7 0.8 %copy-start.2 = (s32[256,64]{0,1:T(8,128)S(1)}, s32[256,64]{0,1:T(8,128)}, u32[]{:S(2)}) copy-start(s32[256,64]{0,1:T(8,128)} %param.7) | copy-start | bytes 196612
  4.6 0.7 copy-start.3
  5.2 29.4 %copy-start.5 = (s32[256]{0:T(256)S(1)}, s32[256]{0:T(256)}, u32[]{:S(2)}) copy-start(s32[256]{0:T(256)} %param.9) | copy-start | bytes 3076
  20.8 25.8 %copy-start.4 = (s32[256]{0:T(256)S(1)}, s32[256]{0:T(256)}, u32[]{:S(2)}) copy-start(s32[256]{0:T(256)} %param.10) | copy-start | bytes 3076

commit v4 on v2

--- a/solution.py
+++ b/solution.py
@@ -10,7 +10,7 @@
 MESH = pl.DeviceIdType.MESH
 LANES = 128
 GRAIN = 16
-GROUP = 16
+GROUP = 32
 GRANT = 24 * 1024 * 1024
 COST = pl.CostEstimate(flops=0, bytes_accessed=24 * 1024 * 1024, transcendentals=0)
 CHUNK = 256

time: 73 us -> 69.7 us (0.955)
  Pallas kernels: 63.8 us -> 60.3 us
    pallas_call x1, Pallas kernels: 13.6 us -> 12.1 us  [on_device(): pl.pallas_call(margin_kernel, out_shape=(shape((listed,), i32), shape((li...]
    pallas_call x1, Pallas kernels: 10.6 us -> 9.55 us  [on_device(): pl.pallas_call(functools.partial(gradient_kernel, grains), out_shape=shap...]
    pallas_call x1, Pallas kernels: 20.4 us -> 19.3 us  [on_device(): pl.pallas_call(functools.partial(scatter_kernel, n), out_shape=(shape((ro...]
where the time goes in v4:
time: 69.7 us; the launch traced here: 69.3 us
  Pallas kernels  60.3 us (87%)
  local copies, waits for them, and re-layouts  5.93 us (9%)
  between operations  2.51 us (4%)
    pallas_call x1, Pallas kernels, on_device(): pl.pallas_call(functools.partial(scatter_kernel, n), out_shape=(shape((ro...  19.3 us
    pallas_call x1, Pallas kernels, on_device(): pl.pallas_call(functools.partial(gather_kernel, n), out_shape=shape((n, r...  15.6 us
    pallas_call x1, Pallas kernels, on_device(): pl.pallas_call(margin_kernel, out_shape=(shape((listed,), i32), shape((li...  12.1 us
    pallas_call x1, Pallas kernels, on_device(): pl.pallas_call(functools.partial(gradient_kernel, grains), out_shape=shap...  9.55 us
    unnamed x15, local copies, waits for them, and re-layouts  5.27 us
    pallas_call x1, Pallas kernels, on_device(): pl.pallas_call(functools.partial(residual_kernel, nf), out_shape=(shape((...  3.78 us

profile of v4, /device:TPU:0, one launch (start us, length us, event | category | flops | bytes accessed | tf_op | source)
XLA Modules:
  0.0 69.3 jit_solution(6846787874122256067)
XLA Ops:
  0.6 0.0 copy-start.6
  0.6 0.0 copy-start.2
  0.7 0.9 %copy-done.2 = f32[256,128]{1,0:T(8,128)S(1)} copy-done((f32[256,128]{1,0:T(8,128)S(1)}, f32[256,128]{1,0:T(8,128)}, u32[]{:S(2)}) %copy-start.2) | copy-done | bytes 131096
  1.6 15.6 %shard_map.85 = bf16[8,256,128]{2,1,0:T(8,128)(2,1)S(1)} custom-call(f32[256,128]{1,0:T(8,128)S(1)} %copy-done.2), custom_call_target="tpu_custom_call" | custom-call | bytes 25165824 | tf_op jit(solution)/shard_map/pallas_call | solution.py:274
  17.1 0.0 copy-start
  17.1 2.2 %copy-done = bf16[256,64,128]{2,1,0:T(8,128)(2,1)S(1)} copy-done((bf16[256,64,128]{2,1,0:T(8,128)(2,1)S(1)}, bf16[256,64,128]{2,1,0:T(8,128)(2,1)}, u32[]{:S(2)}) %copy-start) | copy-done | bytes 4194328
  19.3 0.0 copy-start.3
  19.3 0.8 %copy-done.3 = s32[256,64]{0,1:T(8,128)S(1)} copy-done((s32[256,64]{0,1:T(8,128)S(1)}, s32[256,64]{0,1:T(8,128)}, u32[]{:S(2)}) %copy-start.3) | copy-done | bytes 65560
  20.1 0.0 copy-start.4
  20.1 0.7 copy-done.4
  20.8 0.0 copy-start.1
  20.8 0.0 copy-start.5
  20.8 12.1 %shard_map.86 = (s32[1056]{0:T(1024)S(1)}, s32[1056]{0:T(1024)S(1)}, s32[1]{0:T(128)}, s32[1032,128]{1,0:T(8,128)S(1)}, f32[8,256]{1,0:T(8,128)S(1)}) custom-call(s32[256]{0:T(256)S(1)} %bitcast.13, s32[1,256]{1,0:T(1,128)S(1)} %bitcast.14, s32[64,256]{1,0:T(8,128)S(1)} %bitcast.12, bf16[2048,128]{1,0:T(8,128)(2,1)S(1)} %bitcast.10, ...), custom_call_target="tpu_custom_call" | custom-call | bytes 25165824 | tf_op jit(solution)/shard_map/pallas_call | solution.py:285
  32.9 0.0 copy-done.6
  32.9 3.8 %shard_map.87 = (f32[8,256]{1,0:T(8,128)S(1)}, f32[1,256]{1,0:T(1,128)S(1)}, f32[8,128]{1,0:T(8,128)S(1)}) custom-call(f32[8,256]{1,0:T(8,128)S(1)} %get-tuple-element.16.partial_ref, s32[1,256]{1,0:T(1,128)S(1)} %bitcast.16), custom_call_target="tpu_custom_call" | custom-call | bytes 25165824 | tf_op jit(solution)/shard_map/pallas_call | solution.py:301
  36.7 0.0 copy-done.1
  36.7 9.6 %shard_map.88 = bf16[2048,128]{1,0:T(8,128)(2,1)S(1)} custom-call(s32[1056]{0:T(1024)S(1)} %get-tuple-element.13.glist, s32[1056]{0:T(1024)S(1)} %get-tuple-element.14.rlist, s32[1]{0:T(128)} %get-tuple-element.15.nb, f32[1,256]{1,0:T(1,128)S(1)} %get-tuple-element.17.resid, s32[1032,128]{1,0:T(8,128)S(1)} %get-tuple-element.18.idt, ...), custom_call_target="tpu_custom_call" | custom-call | bytes 25165824 | tf_op jit(solution)/shard_map/pallas_call | solution.py:311
  46.3 0.0 copy-done.5
  46.3 19.3 %shard_map.89 = (f32[256,128]{1,0:T(8,128)S(1)}, f32[8,8,128]{2,1,0:T(8,128)S(1)}) custom-call(bf16[8,256,128]{2,1,0:T(8,128)(2,1)S(1)} %bitcast.11, f32[8,256]{1,0:T(8,128)S(1)} %get-tuple-element.19.margin_ref, s32[1,256]{1,0:T(1,128)S(1)} %bitcast.15, f32[8,128]{1,0:T(8,128)S(1)} %get-tuple-element.20.loss_ref), custom_call_target="tpu_custom_call" | custom-call | bytes 25165824 | tf_op jit(solution)/shard_map/pallas_call | solution.py:321
  65.6 0.6 slice_reduce_fusion
  66.9 0.6 reshape_squeeze.3
  67.5 0.7 copy.10
  (1 shorter events, 0.0 us)
Async XLA Ops:
  0.6 32.3 %copy-start.6 = (s32[256]{0:T(256)S(1)}, s32[256]{0:T(256)}, u32[]{:S(2)}) copy-start(s32[256]{0:T(256)} %param.9) | copy-start | bytes 3076
  0.6 0.9 %copy-start.2 = (f32[256,128]{1,0:T(8,128)S(1)}, f32[256,128]{1,0:T(8,128)}, u32[]{:S(2)}) copy-start(f32[256,128]{1,0:T(8,128)} %w_ref.1) | copy-start | bytes 393220
  17.1 2.2 %copy-start = (bf16[256,64,128]{2,1,0:T(8,128)(2,1)S(1)}, bf16[256,64,128]{2,1,0:T(8,128)(2,1)}, u32[]{:S(2)}) copy-start(bf16[256,64,128]{2,1,0:T(8,128)(2,1)} %param.6) | copy-start | bytes 12582916
  19.3 0.8 %copy-start.3 = (s32[256,64]{0,1:T(8,128)S(1)}, s32[256,64]{0,1:T(8,128)}, u32[]{:S(2)}) copy-start(s32[256,64]{0,1:T(8,128)} %param.7) | copy-start | bytes 196612
  20.1 0.7 copy-start.4
  20.8 15.9 %copy-start.1 = (bf16[256,64,128]{2,1,0:T(8,128)(2,1)S(1)}, bf16[256,64,128]{2,1,0:T(8,128)(2,1)}, u32[]{:S(2)}) copy-start(bf16[256,64,128]{2,1,0:T(8,128)(2,1)} %param.6) | copy-start | bytes 12582916
  20.8 25.4 %copy-start.5 = (s32[256]{0:T(256)S(1)}, s32[256]{0:T(256)}, u32[]{:S(2)}) copy-start(s32[256]{0:T(256)} %param.10) | copy-start | bytes 3076
